TPU v7x, 32 devices: a whole 2x2x4 slice. The times are simulated.
32 devices in a mesh: grp: 1, blk: 8 (over z, y), node: 4 (over x, core), pair: 1.
Axes of the slice: x: 2, y: 2, z: 4, core: 2. Of those that a mesh axis runs over, the one named last changes fastest.
Arguments:
- query: bfloat16 [4608, 1280], P(('grp', 'blk', 'node'), 'pair'), may hold values from -600 to 600
- key: bfloat16 [4608, 1280], P(('grp', 'blk', 'node'), 'pair'), may hold values from -25 to 25
- value: bfloat16 [4608, 1280], P(('grp', 'blk', 'node'), 'pair'), may hold values from -6 to 6
- out_weight: bfloat16 [1280, 1280], P('pair'), may hold values from -0.15625 to 0.15625
Outputs:
- mixed: bfloat16 [4608, 1280], P(('grp', 'blk', 'node', 'pair'))
All inputs are finite; a program needn't handle non-finite values.
Results may differ from a plain program's by a relative error of at most 0.011.
Values may be sent and summed in bfloat16 or wider, within the bound.
A program may use at most 128 MiB of HBM per device.

v0:
```python
import functools
import math

import jax
import jax.numpy as jnp
from jax import lax
from jax.experimental import pallas as pl
from jax.experimental.pallas import tpu as pltpu
from jax.sharding import PartitionSpec as P

HD = 64
WIDE = 2 * HD


def groups_of(blk, heads):
    return max(g for g in range(1, blk + 1) if blk % g == 0 and heads % g == 0)


def kernel(
    G, B, N,
    query_ref, key_ref, value_ref, weight_ref, mixed_ref,
    qp, kvp, kvz, qbuf, kvbuf, vbuf, qfull, peaks, accum, opack, oin, attn, weight,
    z_send, z_recv, q_send, q_recv, kv_send, kv_recv, o_send, o_recv, w_sem,
):
    H, R2, _ = qp.shape
    R = kvp.shape[1]
    hg = H // G
    PL = B // G
    inner = PL // N
    NS = kvbuf.shape[0]
    C = math.gcd(H, B)
    blk, node = lax.axis_index("blk"), lax.axis_index("node")
    z = blk // inner
    p = (blk % inner) * N + node
    bf, f32 = jnp.bfloat16, jnp.float32

    load_weight = pltpu.make_async_copy(weight_ref, weight, w_sem)
    load_weight.start()
    barrier = pltpu.get_barrier_semaphore()
    here = blk * N + node

    def greet(d, _):
        other = lax.rem(here + d, B)
        pl.semaphore_signal(
            barrier, inc=1, device_id={"blk": other // N, "node": lax.rem(other, N)},
            device_id_type=pl.DeviceIdType.MESH,
        )
        return 0

    lax.fori_loop(1, B, greet, 0)

    def peer(zz, pp):
        return {"blk": zz * inner + pp // N, "node": pp % N}

    def remote(src, dst, send, recv, zz, pp):
        return pltpu.make_async_remote_copy(
            src_ref=src, dst_ref=dst, send_sem=send, recv_sem=recv,
            device_id=peer(zz, pp), device_id_type=pl.DeviceIdType.MESH,
        )

    half = lax.broadcasted_iota(jnp.int32, (R2, WIDE), 1) < HD
    wide_half = lax.broadcasted_iota(jnp.int32, (R, WIDE), 1) < HD

    for pair in range(H // 2):
        columns = slice(pair * WIDE, (pair + 1) * WIDE)
        block = query_ref[:, columns].astype(f32)
        turned = pltpu.roll(block, HD, 1)
        qp[2 * pair] = jnp.where(half, block[:R2], turned[R2:]).astype(bf)
        qp[2 * pair + 1] = jnp.where(half, turned[:R2], block[R2:]).astype(bf)
    for pair in range(H // 2):
        columns = slice(pair * WIDE, (pair + 1) * WIDE)
        keys = key_ref[:, columns].astype(f32)
        values = value_ref[:, columns].astype(f32)
        kvp[2 * pair] = jnp.where(wide_half, keys, pltpu.roll(values, HD, 1)).astype(bf)
        kvp[2 * pair + 1] = jnp.where(wide_half, pltpu.roll(keys, HD, 1), values).astype(bf)

    pl.semaphore_wait(barrier, B - 1)

    def send_q(i, act):
        row = lax.rem((z + 1) * hg + i, H)
        zz = row // hg
        n = (row - zz * hg) * B + here
        pp = n // H
        u = n - pp * H
        mine = jnp.logical_and(zz == z, pp == p)

        @pl.when(jnp.logical_not(mine))
        def _():
            act(remote(qp.at[row], qbuf.at[u], q_send.at[row], q_recv.at[u], zz, pp))

        return mine, row, u

    def start_q(i, _):
        mine, row, u = send_q(i, lambda c: c.start())

        @pl.when(mine)
        def _():
            pltpu.make_async_copy(qp.at[row], qbuf.at[u], q_recv.at[u]).start()

        return 0

    lax.fori_loop(0, H, start_q, 0)

    def phase1(dz):
        g = lax.rem(z + dz, G)
        return remote(
            kvp.at[pl.ds(g * hg, hg)], kvz.at[dz - 1], z_send.at[dz - 1], z_recv.at[dz - 1], g, p
        )

    for dz in range(1, G):
        phase1(dz).start()

    def first(pp):
        return (pp * H) // B

    def last(pp):
        return (pp * H + H - 1) // B

    def kv_src(s, h):
        return kvp.at[z * hg + h] if s == 0 else kvz.at[s - 1, h]

    def share_kv(s, act):
        b = s * PL + p

        def one(dp, _):
            pp = lax.rem(p + dp, PL)
            for slot in range(NS):
                @pl.when(first(pp) + slot <= last(pp))
                def _():
                    act(remote(
                        kv_src(s, first(pp) + slot), kvbuf.at[slot, b],
                        kv_send.at[s, dp, slot], kv_recv.at[slot, b], z, pp,
                    ))
            return 0

        lax.fori_loop(1, PL, one, 0)

    def own_kv(s):
        b = s * PL + p
        for slot in range(NS):
            @pl.when(first(p) + slot <= last(p))
            def _():
                pltpu.make_async_copy(kv_src(s, first(p) + slot), kvbuf.at[slot, b], kv_recv.at[slot, b]).start()

    start = lambda c: c.start()
    share_kv(0, start)
    own_kv(0)

    scale = 1.0 / math.sqrt(HD)

    def take_q(u, _):
        pltpu.make_async_copy(qbuf.at[u], qbuf.at[u], q_recv.at[u]).wait()
        both = qbuf[u].astype(f32) * scale
        zero = jnp.zeros_like(both)
        qfull[u] = jnp.concatenate(
            [jnp.where(half, both, zero), jnp.where(half, pltpu.roll(both, HD, 1), zero)], axis=0
        ).astype(bf)
        return 0

    def take_kv(low, high):
        for slot in range(NS):
            @pl.when(first(p) + slot <= last(p))
            def _():
                def one(b, _):
                    pltpu.make_async_copy(kvbuf.at[slot, b], kvbuf.at[slot, b], kv_recv.at[slot, b]).wait()
                    vbuf[slot, b] = jnp.where(wide_half, jnp.ones((), bf), kvbuf[slot, b])
                    return 0
                lax.fori_loop(low * PL, high * PL, one, 0)

    def give(u, act):
        n = p * H + u
        h = n // B
        b = n - h * B
        zz, pp = b // PL, lax.rem(b, PL)
        mine = jnp.logical_and(zz == z, pp == p)
        row = z * hg + h

        @pl.when(jnp.logical_not(mine))
        def _():
            act(remote(opack.at[u], oin.at[row], o_send.at[u], o_recv.at[row], zz, pp))

        return mine, row

    def attend(low, high, t):
        slot = (p * H + t * C) // B - first(p)
        keys = kvbuf[slot, low * PL:high * PL].reshape((high - low) * PL * R, WIDE)
        values = vbuf[slot, low * PL:high * PL].reshape((high - low) * PL * R, WIDE)

        def product(c):
            return lax.dot_general(
                qfull[t * C + c], keys, (((1,), (1,)), ((), ())), preferred_element_type=f32
            )

        def soften(c, scores):
            u = t * C + c
            peak = jnp.max(scores, axis=1, keepdims=True)
            if low > 0:
                before = peaks[u]
                peak = jnp.maximum(before[:, :1], peak)
            expo = jnp.exp(scores - peak).astype(bf)
            total = jnp.dot(expo, values, preferred_element_type=f32)
            if low > 0:
                total = total + accum[u] * jnp.exp(before - peak)
            if high < G:
                peaks[u] = jnp.broadcast_to(peak, (R, WIDE))
                accum[u] = total
                return
            turned = pltpu.roll(total, HD, 1)
            opack[u] = jnp.where(
                half, turned[:R2] / total[:R2], total[R2:] / turned[R2:]
            ).astype(bf)

        scores = product(0)
        for c in range(C):
            ahead = product(c + 1) if c + 1 < C else None
            soften(c, scores)
            scores = ahead
        if high < G:
            return
        for i in range(C):
            u = t * C + i
            mine, row = give(u, start)

            @pl.when(mine)
            def _():
                pltpu.make_async_copy(opack.at[u], oin.at[row], o_recv.at[row]).start()

    def relay(s):
        if s < G:
            phase1(s).wait_recv()
            share_kv(s, start)
            own_kv(s)

    stages = [(s, s + 1) for s in range(min(G, 2))]
    stages += [(s, min(s + 2, G)) for s in range(2, G, 2)]
    turns = H // C
    relay(1)
    lax.fori_loop(0, H, take_q, 0)
    for low, high in stages:
        take_kv(low, high)

        def turn(t, _):
            attend(low, high, t)
            return 0

        if high == 2 and low == 1 and G > 3:
            lax.fori_loop(0, turns // 2, turn, 0)
            relay(3)
            lax.fori_loop(turns // 2, turns, turn, 0)
        else:
            lax.fori_loop(0, turns, turn, 0)
        if high == 1:
            relay(2)
        if high >= 2:
            for s in range(high + 2, min(high + 4, G)):
                relay(s)

    for dz in range(1, G):
        phase1(dz).wait_send()
    for s in range(G):
        share_kv(s, lambda c: c.wait_send())

    def end_q(i, _):
        send_q(i, lambda c: c.wait_send())
        return 0

    lax.fori_loop(0, H, end_q, 0)

    def end(u, _):
        give(u, lambda c: c.wait_send())
        pltpu.make_async_copy(oin.at[u], oin.at[u], o_recv.at[u]).wait()
        return 0

    load_weight.wait()
    lax.fori_loop(0, H, end, 0)
    for pair in range(H // 2):
        even, odd = oin[2 * pair].astype(f32), oin[2 * pair + 1].astype(f32)
        attn[:, pair * WIDE:(pair + 1) * WIDE] = jnp.concatenate(
            [
                jnp.where(half, even, pltpu.roll(odd, HD, 1)),
                jnp.where(half, pltpu.roll(even, HD, 1), odd),
            ],
            axis=0,
        ).astype(bf)
    mixed_ref[...] = jnp.dot(attn[...], weight[...], preferred_element_type=f32).astype(bf)


def per_device(query, key, value, out_weight):
    R, features = query.shape
    H = features // HD
    R2 = R // 2
    nblk, N = lax.axis_size("blk"), lax.axis_size("node")
    B = nblk * N
    G = groups_of(nblk, H)
    hg = H // G
    NS = (H + B - 2) // B + 1
    dma = pltpu.SemaphoreType.DMA
    bf, f32 = jnp.bfloat16, jnp.float32
    vmem = pl.BlockSpec(memory_space=pltpu.VMEM)
    mixed = pl.pallas_call(
        functools.partial(kernel, G, B, N),
        out_shape=jax.ShapeDtypeStruct((R, out_weight.shape[1]), bf),
        in_specs=[vmem, vmem, vmem, pl.BlockSpec(memory_space=pl.ANY)],
        out_specs=vmem,
        scratch_shapes=[
            pltpu.VMEM((H, R2, WIDE), bf),
            pltpu.VMEM((H, R, WIDE), bf),
            pltpu.VMEM((max(G - 1, 1), hg, R, WIDE), bf),
            pltpu.VMEM((H, R2, WIDE), bf),
            pltpu.VMEM((NS, B, R, WIDE), bf),
            pltpu.VMEM((NS, B, R, WIDE), bf),
            pltpu.VMEM((H, R, WIDE), bf),
            pltpu.VMEM((H, R, WIDE), f32),
            pltpu.VMEM((H, R, WIDE), f32),
            pltpu.VMEM((H, R2, WIDE), bf),
            pltpu.VMEM((H, R2, WIDE), bf),
            pltpu.VMEM((R, features), bf),
            pltpu.VMEM(out_weight.shape, bf),
            dma((max(G - 1, 1),)),
            dma((max(G - 1, 1),)),
            dma((H,)),
            dma((H,)),
            dma((G, B // G, NS)),
            dma((NS, B)),
            dma((H,)),
            dma((H,)),
            dma(()),
        ],
        compiler_params=pltpu.CompilerParams(
            collective_id=0, has_side_effects=True, vmem_limit_bytes=60 * 1024 * 1024
        ),
        name="attention",
    )(query, key, value, out_weight)
    return lax.psum_scatter(mixed, "pair", scatter_dimension=0, tiled=True)


def solution(mesh):
    in_specs = (
        P(("grp", "blk", "node"), "pair"),
        P(("grp", "blk", "node"), "pair"),
        P(("grp", "blk", "node"), "pair"),
        P("pair", None),
    )
    out_specs = P(("grp", "blk", "node", "pair"), None)
    return jax.shard_map(
        per_device, mesh=mesh, in_specs=in_specs, out_specs=out_specs, check_vma=False
    )
```

profile of v0, /device:TPU:0, one launch (start us, length us, event | category | flops | bytes accessed | tf_op | source)
XLA Modules:
  0.0 69.3 jit_solution(14208158169416235444)
XLA Ops:
  0.0 67.5 %attention.1 = bf16[144,1280]{1,0:T(8,128)(2,1)} custom-call(bf16[144,1280]{1,0:T(8,128)(2,1)} %query_ref.1, bf16[144,1280]{1,0:T(8,128)(2,1)} %key_ref.1, bf16[144,1280]{1,0:T(8,128)(2,1)} %value_ref.1, bf16[1280,1280]{1,0:T(8,128)(2,1)} %weight_ref.1), custom_call_target="tpu_custom_call" | custom-call | tf_op jit(solution)/shard_map/attention/pallas_call | solution.py:300
  67.5 1.7 %copy.6 = bf16[144,1280]{1,0:T(8,128)(2,1)} copy(bf16[144,1280]{1,0:T(8,128)(2,1)} %attention.1) | data formatting | bytes 737280
where the time goes:
time: 69.4 us; the launch traced here: 69.3 us
  Pallas kernels  67.5 us (97%)
  local copies, waits for them, and re-layouts  1.75 us (3%)
    pallas_call x1, Pallas kernels, per_device(): pl.pallas_call(functools.partial(kernel, G, B, N), out_shape=jax.ShapeDty...  67.5 us
    unnamed x1, local copies, waits for them, and re-layouts  1.75 us

commit v1 on v0

--- a/solution.py
+++ b/solution.py
@@ -285,6 +285,335 @@
     mixed_ref[...] = jnp.dot(attn[...], weight[...], preferred_element_type=f32).astype(bf)
 
 
+def chip_kernel(
+    G, B, N,
+    query_ref, key_ref, value_ref, weight_ref, mixed_ref,
+    qin, kin, vin, qp, kvp, kv, qbuf, qfull, scored, expos, shift, peaks, accum, opack, oin, attn, weight,
+    in_sem, kv_send, kv_recv, q_send, q_recv, s_send, c_send, c_recv, o_send, o_recv, w_sem,
+):
+    H, R2, _ = qp.shape
+    R = kvp.shape[1]
+    hg = H // G
+    PL = B // G
+    inner = PL // N
+    C = PL // 2
+    blk, node = lax.axis_index("blk"), lax.axis_index("node")
+    z, y = blk // inner, blk % inner
+    x, c = node // 2, node % 2
+    bf, f32 = jnp.bfloat16, jnp.float32
+
+    def column(r):
+        return lax.rem(y + r // 2, 2), lax.rem(x + r % 2, 2)
+
+    def at(dz, r, core=None):
+        yy, xx = column(r)
+        return {
+            "blk": lax.rem(z + dz, G) * inner + yy,
+            "node": xx * 2 + (c if core is None else core),
+        }
+
+    def main_row(dz, r):
+        yy, xx = column(r)
+        return lax.rem(z + dz, G) * hg + yy * 2 + xx
+
+    def last_row(dz):
+        return lax.rem(z + dz, G) * hg + C
+
+    def remote(src, dst, send, recv, peer):
+        return pltpu.make_async_remote_copy(
+            src_ref=src, dst_ref=dst, send_sem=send, recv_sem=recv,
+            device_id=peer, device_id_type=pl.DeviceIdType.MESH,
+        )
+
+    def arrived(ref, sem):
+        pltpu.make_async_copy(ref, ref, sem).wait()
+
+    loads = [
+        pltpu.make_async_copy(ref, buf, in_sem.at[n])
+        for n, (ref, buf) in enumerate(((key_ref, kin), (value_ref, vin), (query_ref, qin)))
+    ]
+    for load in loads:
+        load.start()
+    partner = at(0, 0, 1 - c)
+    pairs = [(dz, r) for dz in range(G) for r in range(C) if dz or r]
+    barrier = pltpu.get_barrier_semaphore()
+    for peer in [partner] + [at(dz, r) for dz, r in pairs]:
+        pl.semaphore_signal(barrier, inc=1, device_id=peer, device_id_type=pl.DeviceIdType.MESH)
+    load_weight = pltpu.make_async_copy(weight_ref, weight, w_sem)
+    load_weight.start()
+
+    peaks[...] = jnp.full(peaks.shape, jnp.finfo(f32).min, f32)
+    accum[...] = jnp.zeros(accum.shape, f32)
+    scored[...] = jnp.full(scored.shape, -jnp.inf, f32)
+    expos[...] = jnp.zeros(expos.shape, bf)
+    shift[...] = jnp.ones(shift.shape, f32)
+    half = lax.broadcasted_iota(jnp.int32, (R2, WIDE), 1) < HD
+    wide_half = lax.broadcasted_iota(jnp.int32, (R, WIDE), 1) < HD
+
+    loads[0].wait()
+    loads[1].wait()
+    for pair in range(H // 2):
+        columns = slice(pair * WIDE, (pair + 1) * WIDE)
+        keys = kin[:, columns].astype(f32)
+        values = vin[:, columns].astype(f32)
+        kvp[2 * pair] = jnp.where(wide_half, keys, pltpu.roll(values, HD, 1)).astype(bf)
+        kvp[2 * pair + 1] = jnp.where(wide_half, pltpu.roll(keys, HD, 1), values).astype(bf)
+    loads[2].wait()
+    for pair in range(H // 2):
+        columns = slice(pair * WIDE, (pair + 1) * WIDE)
+        block = qin[:, columns].astype(f32)
+        turned = pltpu.roll(block, HD, 1)
+        qp[2 * pair] = jnp.where(half, block[:R2], turned[R2:]).astype(bf)
+        qp[2 * pair + 1] = jnp.where(half, turned[:R2], block[R2:]).astype(bf)
+    kv[0, 0, 0, 0] = kvp[main_row(0, 0)]
+    kv[1, 0, 0, 0] = kvp[last_row(0)]
+    qbuf[0, 0] = qp[main_row(0, 0)]
+    qbuf[G, 0] = qp[last_row(0)]
+
+    pl.semaphore_wait(barrier, len(pairs) + 1)
+
+    def send_kv(dz, r):
+        return remote(kvp.at[main_row(dz, r)], kv.at[0, dz, 0, r], kv_send.at[0], kv_recv.at[0, dz, r], at(dz, r))
+
+    def send_q(dz, r):
+        return remote(qp.at[main_row(dz, r)], qbuf.at[dz, r], q_send.at[0], q_recv.at[dz, r], at(dz, r))
+
+    def share(s):
+        for r in range(1, C):
+            remote(kv.at[1, s, 0, 0], kv.at[1, s, 0, r], s_send, kv_recv.at[1, s, r], at(0, r)).start()
+
+    for r in range(1, C):
+        send_kv(0, r).start()
+    share(0)
+    for dz in range(1, G):
+        remote(kvp.at[last_row(dz)], kv.at[1, dz, 0, 0], kv_send.at[1], kv_recv.at[1, dz, 0], at(dz, 0)).start()
+    for dz in range(1, G):
+        remote(qp.at[last_row(dz)], qbuf.at[G, dz], q_send.at[1], q_recv.at[G, dz], at(dz, 0)).start()
+    for r in range(1, C):
+        send_q(0, r).start()
+    for dz in range(1, G):
+        for r in range(C):
+            send_kv(dz, r).start()
+    for dz in range(1, G):
+        for r in range(C):
+            send_q(dz, r).start()
+
+    def cross(kind, s):
+        for r in range(C):
+            if not isinstance(s, int) or s or r:
+                arrived(kv.at[kind, s, 0, r], kv_recv.at[kind, s, r])
+        remote(kv.at[kind, s, 0], kv.at[kind, s, 1], c_send.at[kind], c_recv.at[kind, s], partner).start()
+
+    def spread(s):
+        arrived(kv.at[1, s, 0, 0], kv_recv.at[1, s, 0])
+        share(s)
+
+    def cross_shared(s):
+        for r in range(1, C):
+            arrived(kv.at[1, s, 0, r], kv_recv.at[1, s, r])
+        remote(kv.at[1, s, 0], kv.at[1, s, 1], c_send.at[1], c_recv.at[1, s], partner).start()
+
+    scale = 1.0 / math.sqrt(HD)
+
+    def widen(u, b):
+        both = qbuf[u, b].astype(f32) * scale
+        zero = jnp.zeros_like(both)
+        qfull[b] = jnp.concatenate(
+            [jnp.where(half, both, zero), jnp.where(half, pltpu.roll(both, HD, 1), zero)], axis=0
+        ).astype(bf)
+
+    def give(u, b):
+        last = u == G
+        plane = lax.rem(z + G - jnp.where(last, b, u), G)
+        yy, xx = column(b)
+        row = jnp.where(last, last_row(0), main_row(0, 0))
+        return remote(
+            opack.at[u, b], oin.at[row], o_send.at[u], o_recv.at[row],
+            {
+                "blk": plane * inner + jnp.where(last, y, yy),
+                "node": jnp.where(last, x, xx) * 2 + c,
+            },
+        )
+
+    PART = C // 2
+    M = PART * R
+    first_half = lax.broadcasted_iota(jnp.int32, (PL * R, WIDE), 1) < HD
+
+    def unit(t):
+        t = jnp.maximum(t, 0)
+        return lax.rem(t // G + G, G + 1), t % G
+
+    def keys_of(u, s):
+        return kv[u // G, s].reshape(PL * R, WIDE)
+
+    def values_of(u, s):
+        return jnp.where(first_half, jnp.ones((), bf), keys_of(u, s))
+
+    def product(part, keys):
+        return lax.dot_general(
+            qfull[part * PART:(part + 1) * PART].reshape(M, WIDE), keys,
+            (((1,), (1,)), ((), ())), preferred_element_type=f32,
+        )
+
+    def soften(part, u):
+        rows = slice(part * M, (part + 1) * M)
+        scores = scored[part]
+        before = peaks[u, rows]
+        peak = jnp.maximum(before, jnp.max(scores, axis=1, keepdims=True))
+        peaks[u, rows] = peak
+        shift[part] = jnp.exp(before - peak)
+        expos[part] = jnp.exp(scores - peak[:, :1]).astype(bf)
+
+    def gather(part, u, values):
+        rows = slice(part * M, (part + 1) * M)
+        total = jnp.dot(expos[part], values, preferred_element_type=f32)
+        accum[u, rows] = total + accum[u, rows] * shift[part]
+
+    def finish(u, b):
+        total = accum[u, b * R:(b + 1) * R]
+        turned = pltpu.roll(total, HD, 1)
+        opack[u, b] = jnp.where(
+            half, turned[:R2] / total[:R2], total[R2:] / turned[R2:]
+        ).astype(bf)
+        if b:
+            give(u, b).start()
+        else:
+            stays = jnp.logical_or(u == 0, u == G)
+
+            @pl.when(stays)
+            def _():
+                oin[jnp.where(u == G, last_row(0), main_row(0, 0))] = opack[u, 0]
+
+            @pl.when(jnp.logical_not(stays))
+            def _():
+                give(u, 0).start()
+
+    cross(0, 0)
+    cross_shared(0)
+    for s in range(1, G):
+        spread(s)
+    for s in range(1, G):
+        cross_shared(s)
+
+    def tick(t, _):
+        u, s = unit(t)
+        v, w = unit(t - 1)
+        for n in range(1, G):
+            @pl.when(t == G + n)
+            def _():
+                cross(0, n)
+
+        @pl.when(jnp.logical_or(u == 0, u == G))
+        def _():
+            arrived(kv.at[u // G, s, 1], c_recv.at[u // G, s])
+
+        @pl.when(s == 0)
+        def _():
+            for b in range(C):
+                @pl.when(jnp.logical_or(b > 0, jnp.logical_and(u > 0, u < G)))
+                def _():
+                    arrived(qbuf.at[u, b], q_recv.at[u, b])
+                widen(u, b)
+
+        keys, values = keys_of(u, s), values_of(v, w)
+        gather(0, v, values)
+        scored[0] = product(0, keys)
+        soften(1, v)
+        scored[1] = product(1, keys)
+        gather(1, v, values)
+        soften(0, u)
+
+        @pl.when(jnp.logical_and(t > 0, w == G - 1))
+        def _():
+            for b in range(C):
+                finish(v, b)
+
+        return 0
+
+    units = (G + 1) * G
+    lax.fori_loop(0, units, tick, 0)
+    v, w = unit(units - 1)
+    values = values_of(v, w)
+    gather(0, v, values)
+    soften(1, v)
+    for b in range(PART):
+        finish(v, b)
+    gather(1, v, values)
+    for b in range(PART, C):
+        finish(v, b)
+
+    arrived(kvp.at[0:len(pairs)], kv_send.at[0])
+    arrived(kvp.at[0:G - 1], kv_send.at[1])
+    arrived(qp.at[0:len(pairs)], q_send.at[0])
+    arrived(qp.at[0:G - 1], q_send.at[1])
+    arrived(kvp.at[0:G * (C - 1)], s_send)
+    for kind in range(2):
+        arrived(kvp.at[0:G * C], c_send.at[kind])
+    for u in range(G + 1):
+        arrived(qp.at[0:C - (1 if u in (0, G) else 0)], o_send.at[u])
+    for dz, r in pairs:
+        arrived(oin.at[main_row(dz, r)], o_recv.at[main_row(dz, r)])
+    for dz in range(1, G):
+        arrived(oin.at[last_row(dz)], o_recv.at[last_row(dz)])
+    load_weight.wait()
+    for pair in range(H // 2):
+        even, odd = oin[2 * pair].astype(f32), oin[2 * pair + 1].astype(f32)
+        attn[:, pair * WIDE:(pair + 1) * WIDE] = jnp.concatenate(
+            [
+                jnp.where(half, even, pltpu.roll(odd, HD, 1)),
+                jnp.where(half, pltpu.roll(even, HD, 1), odd),
+            ],
+            axis=0,
+        ).astype(bf)
+    mixed_ref[...] = jnp.dot(attn[...], weight[...], preferred_element_type=f32).astype(bf)
+
+
+def chip_call(query, key, value, out_weight, G, B, N):
+    R, features = query.shape
+    H = features // HD
+    R2 = R // 2
+    C = B // G // 2
+    dma = pltpu.SemaphoreType.DMA
+    bf, f32 = jnp.bfloat16, jnp.float32
+    anywhere = pl.BlockSpec(memory_space=pl.ANY)
+    return pl.pallas_call(
+        functools.partial(chip_kernel, G, B, N),
+        out_shape=jax.ShapeDtypeStruct((R, out_weight.shape[1]), bf),
+        in_specs=[anywhere] * 4,
+        out_specs=pl.BlockSpec(memory_space=pltpu.VMEM),
+        scratch_shapes=[
+            pltpu.VMEM((R, features), bf),
+            pltpu.VMEM((R, features), bf),
+            pltpu.VMEM((R, features), bf),
+            pltpu.VMEM((H, R2, WIDE), bf),
+            pltpu.VMEM((H, R, WIDE), bf),
+            pltpu.VMEM((2, G, 2, C, R, WIDE), bf),
+            pltpu.VMEM((G + 1, C, R2, WIDE), bf),
+            pltpu.VMEM((C, R, WIDE), bf),
+            pltpu.VMEM((2, C // 2 * R, B // G * R), f32),
+            pltpu.VMEM((2, C // 2 * R, B // G * R), bf),
+            pltpu.VMEM((2, C // 2 * R, WIDE), f32),
+            pltpu.VMEM((G + 1, C * R, WIDE), f32),
+            pltpu.VMEM((G + 1, C * R, WIDE), f32),
+            pltpu.VMEM((G + 1, C, R2, WIDE), bf),
+            pltpu.VMEM((H, R2, WIDE), bf),
+            pltpu.VMEM((R, features), bf),
+            pltpu.VMEM(out_weight.shape, bf),
+            dma((3,)),
+            dma((2,)), dma((2, G, C)),
+            dma((2,)), dma((G + 1, C)),
+            dma(()),
+            dma((2,)), dma((2, G)),
+            dma((G + 1,)), dma((H,)),
+            dma(()),
+        ],
+        compiler_params=pltpu.CompilerParams(
+            collective_id=0, has_side_effects=True, vmem_limit_bytes=60 * 1024 * 1024
+        ),
+        name="attention",
+    )(query, key, value, out_weight)
+
+
 def per_device(query, key, value, out_weight):
     R, features = query.shape
     H = features // HD
@@ -297,6 +626,9 @@
     dma = pltpu.SemaphoreType.DMA
     bf, f32 = jnp.bfloat16, jnp.float32
     vmem = pl.BlockSpec(memory_space=pltpu.VMEM)
+    if G == N and nblk == 2 * G and hg == G + 1 and R % 16 == 0:
+        mixed = chip_call(query, key, value, out_weight, G, B, N)
+        return lax.psum_scatter(mixed, "pair", scatter_dimension=0, tiled=True)
     mixed = pl.pallas_call(
         functools.partial(kernel, G, B, N),
         out_shape=jax.ShapeDtypeStruct((R, out_weight.shape[1]), bf),

time: 69.4 us -> 59.9 us (0.86)
  Pallas kernels: 67.5 us -> 58 us
    pallas_call x1, Pallas kernels: 67.5 us -> 58 us  [chip_call(): pl.pallas_call(functools.partial(chip_kernel, G, B, N), out_shape=jax.Sha...]
where the time goes in v1:
time: 59.9 us; the launch traced here: 59.8 us
  Pallas kernels  58 us (97%)
  local copies, waits for them, and re-layouts  1.75 us (3%)
    pallas_call x1, Pallas kernels, chip_call(): pl.pallas_call(functools.partial(chip_kernel, G, B, N), out_shape=jax.Sha...  58 us
    unnamed x1, local copies, waits for them, and re-layouts  1.75 us

profile of v1, /device:TPU:0, one launch (start us, length us, event | category | flops | bytes accessed | tf_op | source)
XLA Modules:
  0.0 59.8 jit_solution(15995521995861788890)
XLA Ops:
  0.0 58.0 %attention.1 = bf16[144,1280]{1,0:T(8,128)(2,1)} custom-call(bf16[144,1280]{1,0:T(8,128)(2,1)} %query_ref.1, bf16[144,1280]{1,0:T(8,128)(2,1)} %key_ref.1, bf16[144,1280]{1,0:T(8,128)(2,1)} %value_ref.1, bf16[1280,1280]{1,0:T(8,128)(2,1)} %weight_ref.1), custom_call_target="tpu_custom_call" | custom-call | tf_op jit(solution)/shard_map/attention/pallas_call | solution.py:579
  58.0 1.7 %copy.6 = bf16[144,1280]{1,0:T(8,128)(2,1)} copy(bf16[144,1280]{1,0:T(8,128)(2,1)} %attention.1) | data formatting | bytes 737280

commit v2 on v1

--- a/solution.py
+++ b/solution.py
@@ -384,41 +384,43 @@
 
     for r in range(1, C):
         send_kv(0, r).start()
-    share(0)
-    for dz in range(1, G):
-        remote(kvp.at[last_row(dz)], kv.at[1, dz, 0, 0], kv_send.at[1], kv_recv.at[1, dz, 0], at(dz, 0)).start()
-    for dz in range(1, G):
-        remote(qp.at[last_row(dz)], qbuf.at[G, dz], q_send.at[1], q_recv.at[G, dz], at(dz, 0)).start()
     for r in range(1, C):
         send_q(0, r).start()
-    for dz in range(1, G):
-        for r in range(C):
-            send_kv(dz, r).start()
+    share(0)
     for dz in range(1, G):
         for r in range(C):
             send_q(dz, r).start()
+    for dz in range(1, G):
+        remote(qp.at[last_row(dz)], qbuf.at[G, dz], q_send.at[1], q_recv.at[G, dz], at(dz, 0)).start()
+    def send_near():
+        for dz in range(1, G, 2):
+            for r in range(C):
+                send_kv(dz, r).start()
+
+    def send_shared():
+        for dz in range(1, G):
+            remote(kvp.at[last_row(dz)], kv.at[1, dz, 0, 0], kv_send.at[1], kv_recv.at[1, dz, 0], at(dz, 0)).start()
+
+    def send_far():
+        for dz in range(2, G, 2):
+            for r in range(C):
+                send_kv(dz, r).start()
 
     def cross(kind, s):
-        for r in range(C):
-            if not isinstance(s, int) or s or r:
-                arrived(kv.at[kind, s, 0, r], kv_recv.at[kind, s, r])
+        for r in range(1 if kind or not s else 0, C):
+            arrived(kv.at[kind, s, 0, r], kv_recv.at[kind, s, r])
         remote(kv.at[kind, s, 0], kv.at[kind, s, 1], c_send.at[kind], c_recv.at[kind, s], partner).start()
 
     def spread(s):
         arrived(kv.at[1, s, 0, 0], kv_recv.at[1, s, 0])
         share(s)
 
-    def cross_shared(s):
-        for r in range(1, C):
-            arrived(kv.at[1, s, 0, r], kv_recv.at[1, s, r])
-        remote(kv.at[1, s, 0], kv.at[1, s, 1], c_send.at[1], c_recv.at[1, s], partner).start()
-
     scale = 1.0 / math.sqrt(HD)
 
     def widen(u, b):
         both = qbuf[u, b].astype(f32) * scale
         zero = jnp.zeros_like(both)
-        qfull[b] = jnp.concatenate(
+        qfull[u, b] = jnp.concatenate(
             [jnp.where(half, both, zero), jnp.where(half, pltpu.roll(both, HD, 1), zero)], axis=0
         ).astype(bf)
 
@@ -439,9 +441,23 @@
     M = PART * R
     first_half = lax.broadcasted_iota(jnp.int32, (PL * R, WIDE), 1) < HD
 
+    planes_order = [0] + list(range(1, G, 2)) + list(range(2, G, 2))
+    order = [0] + list(range(1, G, 2)) + [G] + list(range(2, G, 2))
+    MID = order.index(G)
+
+    def pick(index, values):
+        found = values[-1]
+        for n, value in enumerate(values[:-1]):
+            found = jnp.where(index == n, value, found)
+        return found
+
     def unit(t):
         t = jnp.maximum(t, 0)
-        return lax.rem(t // G + G, G + 1), t % G
+        k, m = t // G, t % G
+        late = pick(m, list(range(2, G, 2)) + list(range(1, G, 2)) + [0])
+        u = jnp.where(k == MID, G, jnp.where(k == G, late, m))
+        s = jnp.where(k == MID, pick(m, planes_order), pick(k, order))
+        return k, u, s
 
     def keys_of(u, s):
         return kv[u // G, s].reshape(PL * R, WIDE)
@@ -449,9 +465,9 @@
     def values_of(u, s):
         return jnp.where(first_half, jnp.ones((), bf), keys_of(u, s))
 
-    def product(part, keys):
+    def product(part, u, keys):
         return lax.dot_general(
-            qfull[part * PART:(part + 1) * PART].reshape(M, WIDE), keys,
+            qfull[u, part * PART:(part + 1) * PART].reshape(M, WIDE), keys,
             (((1,), (1,)), ((), ())), preferred_element_type=f32,
         )
 
@@ -469,93 +485,121 @@
         total = jnp.dot(expos[part], values, preferred_element_type=f32)
         accum[u, rows] = total + accum[u, rows] * shift[part]
 
-    def finish(u, b):
+    def divide(u, b):
         total = accum[u, b * R:(b + 1) * R]
         turned = pltpu.roll(total, HD, 1)
-        opack[u, b] = jnp.where(
-            half, turned[:R2] / total[:R2], total[R2:] / turned[R2:]
-        ).astype(bf)
+        above = jnp.where(half, turned[:R2], total[R2:])
+        below = jnp.where(half, total[:R2], turned[R2:])
+        opack[u, b] = (above / below).astype(bf)
+
+    def deliver(u, b):
         if b:
             give(u, b).start()
-        else:
-            stays = jnp.logical_or(u == 0, u == G)
-
-            @pl.when(stays)
+            return
+        stays = jnp.logical_or(u == 0, u == G)
+
+        @pl.when(stays)
+        def _():
+            oin[jnp.where(u == G, last_row(0), main_row(0, 0))] = opack[u, 0]
+
+        @pl.when(jnp.logical_not(stays))
+        def _():
+            give(u, 0).start()
+
+    inside = jnp.logical_and(z > 0, z < G - 1)
+
+    @pl.when(inside)
+    def _():
+        send_near()
+        send_shared()
+        send_far()
+
+    cross(0, 0)
+
+    @pl.when(jnp.logical_not(inside))
+    def _():
+        send_near()
+
+    stages = {4: send_shared, 8: send_far}
+    steps = {
+        3: [(cross, 0, 1)],
+        6: [(cross, 0, 3), (cross, 1, 0)],
+        8: [(spread, 1)],
+        9: [(spread, 3)],
+        11: [(spread, 2)],
+        12: [(cross, 1, 1)],
+        13: [(cross, 1, 3)],
+        14: [(cross, 1, 2)],
+        15: [(cross, 0, 2)],
+    }
+
+    def tick(t, _, ending=False):
+        k, u, s = unit(t)
+        j, v, w = unit(t - 1)
+        if not ending:
+            for n, stage in stages.items():
+                pl.when(jnp.logical_and(t == n, jnp.logical_not(inside)))(stage)
+            for n, step in steps.items():
+                @pl.when(t == n)
+                def _():
+                    for act, *where in step:
+                        act(*where)
+
+            @pl.when(jnp.logical_or(k == MID, t % G == 0))
             def _():
-                oin[jnp.where(u == G, last_row(0), main_row(0, 0))] = opack[u, 0]
-
-            @pl.when(jnp.logical_not(stays))
+                arrived(kv.at[u // G, s, 1], c_recv.at[u // G, s])
+
+            @pl.when(jnp.logical_or(k == 0, t == MID * G))
             def _():
-                give(u, 0).start()
-
-    cross(0, 0)
-    cross_shared(0)
-    for s in range(1, G):
-        spread(s)
-    for s in range(1, G):
-        cross_shared(s)
-
-    def tick(t, _):
-        u, s = unit(t)
-        v, w = unit(t - 1)
-        for n in range(1, G):
-            @pl.when(t == G + n)
-            def _():
-                cross(0, n)
-
-        @pl.when(jnp.logical_or(u == 0, u == G))
-        def _():
-            arrived(kv.at[u // G, s, 1], c_recv.at[u // G, s])
-
-        @pl.when(s == 0)
+                for b in range(C):
+                    @pl.when(jnp.logical_or(b > 0, jnp.logical_and(u > 0, u < G)))
+                    def _():
+                        arrived(qbuf.at[u, b], q_recv.at[u, b])
+                    widen(u, b)
+
+        keys, values = keys_of(u, s), values_of(v, w)
+        gather(0, v, values)
+        scored[0] = product(0, u, keys)
+        soften(1, v)
+        scored[1] = product(1, u, keys)
+        gather(1, v, values)
+        if ending:
+            for b in range(C):
+                divide(v, b)
+        soften(0, u)
+        if ending:
+            for b in range(C):
+                deliver(v, b)
+            return 0
+
+        @pl.when(t == (MID + 1) * G)
         def _():
             for b in range(C):
-                @pl.when(jnp.logical_or(b > 0, jnp.logical_and(u > 0, u < G)))
-                def _():
-                    arrived(qbuf.at[u, b], q_recv.at[u, b])
-                widen(u, b)
-
-        keys, values = keys_of(u, s), values_of(v, w)
-        gather(0, v, values)
-        scored[0] = product(0, keys)
-        soften(1, v)
-        scored[1] = product(1, keys)
-        gather(1, v, values)
-        soften(0, u)
-
-        @pl.when(jnp.logical_and(t > 0, w == G - 1))
-        def _():
-            for b in range(C):
-                finish(v, b)
+                divide(v, b)
+                deliver(v, b)
 
         return 0
 
     units = (G + 1) * G
-    lax.fori_loop(0, units, tick, 0)
-    v, w = unit(units - 1)
+    lax.fori_loop(0, units - G + 1, tick, 0)
+    lax.fori_loop(units - G + 1, units, functools.partial(tick, ending=True), 0)
+    j, v, w = unit(units - 1)
     values = values_of(v, w)
     gather(0, v, values)
     soften(1, v)
     for b in range(PART):
-        finish(v, b)
+        divide(v, b)
+        deliver(v, b)
     gather(1, v, values)
     for b in range(PART, C):
-        finish(v, b)
-
-    arrived(kvp.at[0:len(pairs)], kv_send.at[0])
-    arrived(kvp.at[0:G - 1], kv_send.at[1])
-    arrived(qp.at[0:len(pairs)], q_send.at[0])
-    arrived(qp.at[0:G - 1], q_send.at[1])
-    arrived(kvp.at[0:G * (C - 1)], s_send)
-    for kind in range(2):
-        arrived(kvp.at[0:G * C], c_send.at[kind])
-    for u in range(G + 1):
-        arrived(qp.at[0:C - (1 if u in (0, G) else 0)], o_send.at[u])
+        divide(v, b)
+        deliver(v, b)
+
+    load_weight.wait()
+    for dz in range(1, G):
+        arrived(oin.at[last_row(dz)], o_recv.at[last_row(dz)])
     for dz, r in pairs:
         arrived(oin.at[main_row(dz, r)], o_recv.at[main_row(dz, r)])
-    for dz in range(1, G):
-        arrived(oin.at[last_row(dz)], o_recv.at[last_row(dz)])
-    load_weight.wait()
     for pair in range(H // 2):
         even, odd = oin[2 * pair].astype(f32), oin[2 * pair + 1].astype(f32)
         attn[:, pair * WIDE:(pair + 1) * WIDE] = jnp.concatenate(
@@ -566,6 +610,16 @@
             axis=0,
         ).astype(bf)
     mixed_ref[...] = jnp.dot(attn[...], weight[...], preferred_element_type=f32).astype(bf)
+
+    arrived(kvp.at[0:len(pairs)], kv_send.at[0])
+    arrived(kvp.at[0:G - 1], kv_send.at[1])
+    arrived(qp.at[0:len(pairs)], q_send.at[0])
+    arrived(qp.at[0:G - 1], q_send.at[1])
+    arrived(kvp.at[0:G * (C - 1)], s_send)
+    for kind in range(2):
+        arrived(kvp.at[0:G * C], c_send.at[kind])
+    for u in range(G + 1):
+        arrived(qp.at[0:C - (1 if u in (0, G) else 0)], o_send.at[u])
 
 
 def chip_call(query, key, value, out_weight, G, B, N):
@@ -589,7 +643,7 @@
             pltpu.VMEM((H, R, WIDE), bf),
             pltpu.VMEM((2, G, 2, C, R, WIDE), bf),
             pltpu.VMEM((G + 1, C, R2, WIDE), bf),
-            pltpu.VMEM((C, R, WIDE), bf),
+            pltpu.VMEM((G + 1, C, R, WIDE), bf),
             pltpu.VMEM((2, C // 2 * R, B // G * R), f32),
             pltpu.VMEM((2, C // 2 * R, B // G * R), bf),
             pltpu.VMEM((2, C // 2 * R, WIDE), f32),

time: 59.9 us -> 52.2 us (0.87)
  Pallas kernels: 58 us -> 50.3 us
    pallas_call x1, Pallas kernels: 58 us -> 50.3 us  [chip_call(): pl.pallas_call(functools.partial(chip_kernel, G, B, N), out_shape=jax.Sha...]
where the time goes in v2:
time: 52.2 us; the launch traced here: 52.1 us
  Pallas kernels  50.3 us (96%)
  local copies, waits for them, and re-layouts  1.75 us (3%)
    pallas_call x1, Pallas kernels, chip_call(): pl.pallas_call(functools.partial(chip_kernel, G, B, N), out_shape=jax.Sha...  50.3 us
    unnamed x1, local copies, waits for them, and re-layouts  1.75 us

profile of v2, /device:TPU:0, one launch (start us, length us, event | category | flops | bytes accessed | tf_op | source)
XLA Modules:
  0.0 52.1 jit_solution(13244388382052593596)
XLA Ops:
  0.0 50.3 %attention.1 = bf16[144,1280]{1,0:T(8,128)(2,1)} custom-call(bf16[144,1280]{1,0:T(8,128)(2,1)} %query_ref.1, bf16[144,1280]{1,0:T(8,128)(2,1)} %key_ref.1, bf16[144,1280]{1,0:T(8,128)(2,1)} %value_ref.1, bf16[1280,1280]{1,0:T(8,128)(2,1)} %weight_ref.1), custom_call_target="tpu_custom_call" | custom-call | tf_op jit(solution)/shard_map/attention/pallas_call | solution.py:633
  50.4 1.7 %copy.6 = bf16[144,1280]{1,0:T(8,128)(2,1)} copy(bf16[144,1280]{1,0:T(8,128)(2,1)} %attention.1) | data formatting | bytes 737280

commit v3 on v2

--- a/solution.py
+++ b/solution.py
@@ -407,7 +407,7 @@
                 send_kv(dz, r).start()
 
     def cross(kind, s):
-        for r in range(1 if kind or not s else 0, C):
+        for r in range(1 if kind or isinstance(s, int) and s == 0 else 0, C):
             arrived(kv.at[kind, s, 0, r], kv_recv.at[kind, s, r])
         remote(kv.at[kind, s, 0], kv.at[kind, s, 1], c_send.at[kind], c_recv.at[kind, s], partner).start()
 
@@ -442,8 +442,9 @@
     first_half = lax.broadcasted_iota(jnp.int32, (PL * R, WIDE), 1) < HD
 
     planes_order = [0] + list(range(1, G, 2)) + list(range(2, G, 2))
-    order = [0] + list(range(1, G, 2)) + [G] + list(range(2, G, 2))
-    MID = order.index(G)
+    first = jnp.where(z == G // 2, G - 1, 1)
+    order = [0, first, G - first, G] + list(range(2, G, 2))
+    MID = 3
 
     def pick(index, values):
         found = values[-1]
@@ -451,13 +452,19 @@
             found = jnp.where(index == n, value, found)
         return found
 
-    def unit(t):
-        t = jnp.maximum(t, 0)
-        k, m = t // G, t % G
-        late = pick(m, list(range(2, G, 2)) + list(range(1, G, 2)) + [0])
-        u = jnp.where(k == MID, G, jnp.where(k == G, late, m))
-        s = jnp.where(k == MID, pick(m, planes_order), pick(k, order))
-        return k, u, s
+    def unit(k, m):
+        if k == MID:
+            return G, pick(m, planes_order)
+        if k == G:
+            m = pick(m, list(range(2, G, 2)) + list(range(1, G, 2)) + [0])
+        return m, order[k]
+
+    def before(k, m):
+        u, s = unit(k, jnp.maximum(m - 1, 0))
+        if k == 0:
+            return u, s
+        v, w = unit(k - 1, jnp.int32(G - 1))
+        return jnp.where(m == 0, v, u), jnp.where(m == 0, w, s)
 
     def keys_of(u, s):
         return kv[u // G, s].reshape(PL * R, WIDE)
@@ -522,8 +529,8 @@
 
     stages = {4: send_shared, 8: send_far}
     steps = {
-        3: [(cross, 0, 1)],
-        6: [(cross, 0, 3), (cross, 1, 0)],
+        3: [(cross, 0, first)],
+        6: [(cross, 0, G - first), (cross, 1, 0)],
         8: [(spread, 1)],
         9: [(spread, 3)],
         11: [(spread, 2)],
@@ -533,57 +540,61 @@
         15: [(cross, 0, 2)],
     }
 
-    def tick(t, _, ending=False):
-        k, u, s = unit(t)
-        j, v, w = unit(t - 1)
-        if not ending:
-            for n, stage in stages.items():
-                pl.when(jnp.logical_and(t == n, jnp.logical_not(inside)))(stage)
-            for n, step in steps.items():
-                @pl.when(t == n)
+    def tick(k, m, _, ending=False):
+        u, s = unit(k, m)
+        v, w = before(k, m)
+        for n, stage in stages.items():
+            if n // G == k and not ending:
+                pl.when(jnp.logical_and(m == n % G, jnp.logical_not(inside)))(stage)
+        for n, step in steps.items():
+            if n // G == k and not ending:
+                @pl.when(m == n % G)
                 def _():
                     for act, *where in step:
                         act(*where)
 
-            @pl.when(jnp.logical_or(k == MID, t % G == 0))
-            def _():
-                arrived(kv.at[u // G, s, 1], c_recv.at[u // G, s])
-
-            @pl.when(jnp.logical_or(k == 0, t == MID * G))
+        if not ending:
+            kind = int(k == MID)
+            pl.when(jnp.logical_or(kind == 1, m == 0))(
+                lambda: arrived(kv.at[kind, s, 1], c_recv.at[kind, s])
+            )
+        if k == 0:
+            for b in range(C):
+                @pl.when(jnp.logical_or(b > 0, u > 0))
+                def _():
+                    arrived(qbuf.at[u, b], q_recv.at[u, b])
+                widen(u, b)
+        elif k == MID:
+            @pl.when(m == 0)
             def _():
                 for b in range(C):
-                    @pl.when(jnp.logical_or(b > 0, jnp.logical_and(u > 0, u < G)))
-                    def _():
+                    if b:
                         arrived(qbuf.at[u, b], q_recv.at[u, b])
                     widen(u, b)
 
         keys, values = keys_of(u, s), values_of(v, w)
+        scored[0] = product(0, u, keys)
         gather(0, v, values)
-        scored[0] = product(0, u, keys)
         soften(1, v)
         scored[1] = product(1, u, keys)
+        soften(0, u)
         gather(1, v, values)
         if ending:
             for b in range(C):
                 divide(v, b)
-        soften(0, u)
-        if ending:
             for b in range(C):
                 deliver(v, b)
-            return 0
-
-        @pl.when(t == (MID + 1) * G)
-        def _():
+        elif k == MID + 1:
             for b in range(C):
                 divide(v, b)
                 deliver(v, b)
-
         return 0
 
-    units = (G + 1) * G
-    lax.fori_loop(0, units - G + 1, tick, 0)
-    lax.fori_loop(units - G + 1, units, functools.partial(tick, ending=True), 0)
-    j, v, w = unit(units - 1)
+    for k in range(MID + 1):
+        lax.fori_loop(0, G, functools.partial(tick, k), 0)
+    tick(MID + 1, jnp.int32(0), 0)
+    lax.fori_loop(1, G, functools.partial(tick, MID + 1, ending=True), 0)
+    v, w = unit(MID + 1, jnp.int32(G - 1))
     values = values_of(v, w)
     gather(0, v, values)
     soften(1, v)
@@ -662,7 +673,7 @@
             dma(()),
         ],
         compiler_params=pltpu.CompilerParams(
-            collective_id=0, has_side_effects=True, vmem_limit_bytes=60 * 1024 * 1024
+            collective_id=0, has_side_effects=True, vmem_limit_bytes=54656 * 1024
         ),
         name="attention",
     )(query, key, value, out_weight)

time: 52.2 us -> 49.5 us (0.948)
  Pallas kernels: 50.3 us -> 48.6 us
  local copies, waits for them, and re-layouts: 1.75 us -> 0.74 us
    pallas_call x1, Pallas kernels: 50.3 us -> 48.6 us  [chip_call(): pl.pallas_call(functools.partial(chip_kernel, G, B, N), out_shape=jax.Sha...]
    unnamed x1, local copies, waits for them, and re-layouts: 1.75 us -> 0.74 us
where the time goes in v3:
time: 49.5 us; the launch traced here: 49.3 us
  Pallas kernels  48.6 us (98%)
  local copies, waits for them, and re-layouts  0.74 us (1%)
    pallas_call x1, Pallas kernels, chip_call(): pl.pallas_call(functools.partial(chip_kernel, G, B, N), out_shape=jax.Sha...  48.6 us

profile of v3, /device:TPU:0, one launch (start us, length us, event | category | flops | bytes accessed | tf_op | source)
XLA Modules:
  0.0 49.3 jit_solution(3192303985358142788)
XLA Ops:
  0.0 48.6 %attention.1 = bf16[144,1280]{1,0:T(8,128)(2,1)S(1)} custom-call(bf16[144,1280]{1,0:T(8,128)(2,1)} %query_ref.1, bf16[144,1280]{1,0:T(8,128)(2,1)} %key_ref.1, bf16[144,1280]{1,0:T(8,128)(2,1)} %value_ref.1, bf16[1280,1280]{1,0:T(8,128)(2,1)} %weight_ref.1), custom_call_target="tpu_custom_call" | custom-call | tf_op jit(solution)/shard_map/attention/pallas_call | solution.py:644
  48.6 0.7 %copy.6 = bf16[144,1280]{1,0:T(8,128)(2,1)} copy(bf16[144,1280]{1,0:T(8,128)(2,1)S(1)} %attention.1) | data formatting | bytes 737280

commit v4 on v3

--- a/solution.py
+++ b/solution.py
@@ -531,9 +531,9 @@
     steps = {
         3: [(cross, 0, first)],
         6: [(cross, 0, G - first), (cross, 1, 0)],
-        8: [(spread, 1)],
-        9: [(spread, 3)],
-        11: [(spread, 2)],
+        7: [(spread, 1)],
+        8: [(spread, 3)],
+        9: [(spread, 2)],
         12: [(cross, 1, 1)],
         13: [(cross, 1, 3)],
         14: [(cross, 1, 2)],
@@ -575,15 +575,20 @@
         keys, values = keys_of(u, s), values_of(v, w)
         scored[0] = product(0, u, keys)
         gather(0, v, values)
+        if ending:
+            for b in range(PART):
+                divide(v, b)
         soften(1, v)
+        if ending:
+            for b in range(PART):
+                give(v, b).start()
         scored[1] = product(1, u, keys)
         soften(0, u)
         gather(1, v, values)
         if ending:
-            for b in range(C):
+            for b in range(PART, C):
                 divide(v, b)
-            for b in range(C):
-                deliver(v, b)
+                give(v, b).start()
         elif k == MID + 1:
             for b in range(C):
                 divide(v, b)

time: 49.5 us -> 48.8 us (0.986)
  Pallas kernels: 48.6 us -> 47.9 us
    pallas_call x1, Pallas kernels: 48.6 us -> 47.9 us  [chip_call(): pl.pallas_call(functools.partial(chip_kernel, G, B, N), out_shape=jax.Sha...]
where the time goes in v4:
time: 48.8 us; the launch traced here: 48.6 us
  Pallas kernels  47.9 us (98%)
  local copies, waits for them, and re-layouts  0.74 us (2%)
    pallas_call x1, Pallas kernels, chip_call(): pl.pallas_call(functools.partial(chip_kernel, G, B, N), out_shape=jax.Sha...  47.9 us

profile of v4, /device:TPU:0, one launch (start us, length us, event | category | flops | bytes accessed | tf_op | source)
XLA Modules:
  0.0 48.6 jit_solution(13530070876930062209)
XLA Ops:
  0.0 47.9 %attention.1 = bf16[144,1280]{1,0:T(8,128)(2,1)S(1)} custom-call(bf16[144,1280]{1,0:T(8,128)(2,1)} %query_ref.1, bf16[144,1280]{1,0:T(8,128)(2,1)} %key_ref.1, bf16[144,1280]{1,0:T(8,128)(2,1)} %value_ref.1, bf16[1280,1280]{1,0:T(8,128)(2,1)} %weight_ref.1), custom_call_target="tpu_custom_call" | custom-call | tf_op jit(solution)/shard_map/attention/pallas_call | solution.py:649
  47.9 0.7 %copy.6 = bf16[144,1280]{1,0:T(8,128)(2,1)} copy(bf16[144,1280]{1,0:T(8,128)(2,1)S(1)} %attention.1) | data formatting | bytes 737280

commit v5 on v4

--- a/solution.py
+++ b/solution.py
@@ -386,7 +386,6 @@
         send_kv(0, r).start()
     for r in range(1, C):
         send_q(0, r).start()
-    share(0)
     for dz in range(1, G):
         for r in range(C):
             send_q(dz, r).start()
@@ -522,6 +521,7 @@
         send_far()
 
     cross(0, 0)
+    share(0)
 
     @pl.when(jnp.logical_not(inside))
     def _():

time: 48.8 us -> 48.7 us (level)
  no operation moved by 1% of the time
where the time goes in v5:
time: 48.7 us; the launch traced here: 48.6 us
  Pallas kernels  47.9 us (98%)
  local copies, waits for them, and re-layouts  0.74 us (2%)
    pallas_call x1, Pallas kernels, chip_call(): pl.pallas_call(functools.partial(chip_kernel, G, B, N), out_shape=jax.Sha...  47.9 us

profile of v5, /device:TPU:0, one launch (start us, length us, event | category | flops | bytes accessed | tf_op | source)
XLA Modules:
  0.0 48.6 jit_solution(1806635397482576391)
XLA Ops:
  0.0 47.9 %attention.1 = bf16[144,1280]{1,0:T(8,128)(2,1)S(1)} custom-call(bf16[144,1280]{1,0:T(8,128)(2,1)} %query_ref.1, bf16[144,1280]{1,0:T(8,128)(2,1)} %key_ref.1, bf16[144,1280]{1,0:T(8,128)(2,1)} %value_ref.1, bf16[1280,1280]{1,0:T(8,128)(2,1)} %weight_ref.1), custom_call_target="tpu_custom_call" | custom-call | tf_op jit(solution)/shard_map/attention/pallas_call | solution.py:649
  47.9 0.7 %copy.6 = bf16[144,1280]{1,0:T(8,128)(2,1)} copy(bf16[144,1280]{1,0:T(8,128)(2,1)S(1)} %attention.1) | data formatting | bytes 737280
